TPU v7x, 32 devices: a whole 2x2x4 slice. The times are simulated.
32 devices in a mesh: row: 4 (over z), col: 8 (over y, x, core).
Axes of the slice: x: 2, y: 2, z: 4, core: 2. Of those that a mesh axis runs over, the one named last changes fastest.
Arguments:
- impedance: bfloat16 [2048, 2048], P('row', 'col'), may hold values from -2 to 50
- start: float32 [2048, 32], P(('row', 'col')), may hold values from -6 to 6
Outputs:
- basis: float32 [2048, 288], P(('row', 'col'))
- alphas: float32 [8, 32, 32], replicated
- betas: float32 [8, 32, 32], replicated
All inputs are finite; a program needn't handle non-finite values.
Results may differ from a plain program's by a relative error of at most 0.039.
Values may be sent and summed in bfloat16 or wider, within the bound.
A program may use at most 64 MiB of HBM per device.

v0:
```python
import functools

import jax
import jax.numpy as jnp
from jax import lax
from jax.experimental import pallas as pl
from jax.experimental.pallas import tpu as pltpu
from jax.sharding import PartitionSpec as P

STEPS = 8
LANES = 128
CHUNK = 2048
PANEL = 16
MESH = pl.DeviceIdType.MESH
f32 = jnp.float32
bf16 = jnp.bfloat16


def split(value):
    high = value.astype(bf16)
    return high, (value - high.astype(f32)).astype(bf16)


def across(left, right):
    return lax.dot_general(left, right, (((1,), (1,)), ((), ())), preferred_element_type=f32)


def over(trips, body, init):
    if trips == 1:
        return body(0, init)
    return lax.fori_loop(0, trips, body, init)


def factor(gram):
    width = gram.shape[0]
    rows = lax.broadcasted_iota(jnp.int32, (width, 2 * width), 0)
    lanes = lax.broadcasted_iota(jnp.int32, (width, 2 * width), 1)
    eye = (lanes - width == rows).astype(f32)
    work = jnp.where(lanes < width, jnp.concatenate([gram, gram], axis=1), eye)
    for base in range(0, width, PANEL):
        cols = [
            jnp.broadcast_to(work[:, base + m : base + m + 1], work.shape) for m in range(PANEL)
        ]
        for m in range(PANEL):
            k = base + m
            scale = 1.0 / cols[m][k : k + 1]
            mult = jnp.where(rows > k, cols[m] * scale, 0.0)
            work = work - mult * work[k : k + 1]
            for n in range(m + 1, PANEL):
                cols[n] = cols[n] - mult * cols[n][k : k + 1]
    diagonal = jnp.sum(jnp.where(lanes == rows, work, 0.0), axis=1, keepdims=True)
    work = work * lax.rsqrt(diagonal)
    upper = jnp.where(lanes >= rows, work, 0.0)[:, :width]
    return upper, work[:, width:]


def kernel(
    n_row, n_col, pair,
    imp_ref, st_ref, basis_ref, alpha_ref, beta_ref,
    slab, parts, begin, image, high, low, res,
    a_send, a_recv, p_send, p_recv, s_send, s_recv, i_send, i_recv,
):
    r = lax.axis_index("row")
    c = lax.axis_index("col")
    per_row = n_col // pair
    groups = n_row * per_row
    devices = n_row * n_col
    me = r * n_col + c
    group = r * per_row + c // pair
    member = c % pair
    width = st_ref.shape[0]
    cb = imp_ref.shape[1]
    total = image.shape[2]
    chunk = min(CHUNK, total)
    trips = total // chunk

    barrier = pltpu.get_barrier_semaphore()
    for d in range(1, devices):
        t = (me + d) % devices
        pl.semaphore_signal(barrier, inc=1, device_id=(t // n_col, t % n_col), device_id_type=MESH)
    pl.semaphore_wait(barrier, devices - 1)

    def lane_block(g):
        return pl.ds(pl.multiple_of(g * LANES, LANES), LANES)

    def row_block(k):
        rows = per_row * LANES
        return pl.ds(pl.multiple_of(k * rows, rows), rows)

    def p_copy(q, owner):
        return pltpu.make_async_remote_copy(
            src_ref=st_ref, dst_ref=parts.at[owner],
            send_sem=p_send.at[q], recv_sem=p_recv.at[q],
            device_id=(r, c - member + (member + q) % pair), device_id_type=MESH,
        )

    near = sorted(range(n_row), key=lambda dz: min(dz, n_row - dz))
    slots = {dz: [dz * per_row + dx for dx in range(per_row) if dz or dx] for dz in near}
    near_first = [q for dz in near for q in reversed(slots[dz])]

    def peer(q):
        dz, dx = q // per_row, q % per_row
        return ((r + dz) % n_row, ((c // pair + dx) % per_row) * pair + member)

    def source(q):
        dz, dx = q // per_row, q % per_row
        return ((r + n_row - dz) % n_row) * per_row + (c // pair + per_row - dx) % per_row

    def st_copy(q, owner):
        where = begin.at[:, lane_block(owner)]
        return pltpu.make_async_remote_copy(
            src_ref=where, dst_ref=where, send_sem=s_send.at[q], recv_sem=s_recv.at[q],
            device_id=peer(q), device_id_type=MESH,
        )

    def a_copy(q, owner):
        t = (c + q) % n_col
        return pltpu.make_async_remote_copy(
            src_ref=imp_ref.at[pl.ds(pl.multiple_of((t // pair) * LANES, LANES), LANES), :],
            dst_ref=slab.at[owner],
            send_sem=a_send.at[q], recv_sem=a_recv.at[q],
            device_id=(r, t), device_id_type=MESH,
        )

    for q in range(1, pair):
        p_copy(q, member).start()
    parts[member] = st_ref[...]
    for q in range(1, pair):
        p_copy(q, (member - q + pair) % pair).wait_recv()
    whole = parts[0]
    for p in range(1, pair):
        whole = whole + parts[p]
    begin[:, lane_block(group)] = whole
    for q in near_first:
        st_copy(q, group).start()
    for q in range(1, n_col):
        a_copy(q, c).start()
    slab[c] = imp_ref[pl.ds(pl.multiple_of((c // pair) * LANES, LANES), LANES), :]
    for q in range(1, groups):
        st_copy(q, source(q)).wait_recv()

    def orthonormal(block, index):
        def gram_chunk(i, gram):
            at = pl.ds(pl.multiple_of(i * chunk, chunk), chunk)
            h, l = split(block(at))
            res[0, :, at] = h
            res[1, :, at] = l
            both = across(jnp.concatenate([h, l], axis=0), h)
            return gram + (both[:width] + (both[width:] + both[width:].T))

        gram = over(trips, gram_chunk, jnp.zeros((width, width), f32))
        upper, inverse = factor(gram)
        ih, il = split(inverse)
        wide = jnp.concatenate([ih, ih, il], axis=1)

        def solve_chunk(i, carry):
            at = pl.ds(pl.multiple_of(i * chunk, chunk), chunk)
            h = res[0, :, at]
            tall = jnp.concatenate([h, res[1, :, at], h], axis=0)
            h, l = split(jnp.dot(wide, tall, preferred_element_type=f32))
            high[index * width : (index + 1) * width, at] = h
            low[index * width : (index + 1) * width, at] = l
            return carry

        over(trips, solve_chunk, 0)
        return upper

    def first(at):
        return begin[:, at].astype(f32)

    orthonormal(first, 0)
    for q in range(1, n_col):
        a_copy(q, (c - q + n_col) % n_col).wait_recv()
    for q in range(1, pair):
        p_copy(q, member).wait_send()
    for q in range(1, groups):
        st_copy(q, group).wait_send()
    for q in range(1, n_col):
        a_copy(q, c).wait_send()

    def i_copy(par, q, owner):
        where = image.at[par, :, lane_block(owner)]
        return pltpu.make_async_remote_copy(
            src_ref=where, dst_ref=where,
            send_sem=i_send.at[par, q], recv_sem=i_recv.at[par, q],
            device_id=peer(q), device_id_type=MESH,
        )

    for step in range(STEPS):
        par = step % 2
        seen = (step + 1) * width
        mine = jnp.zeros((width, LANES), f32)
        for k in range(n_col):
            mine = mine + across(high[step * width : seen, k * cb : (k + 1) * cb], slab[k])
        image[par, :, lane_block(group)] = mine.astype(image.dtype)
        for q in near_first:
            i_copy(par, q, group).start()
        coeffs = jnp.zeros((width, seen), f32)
        for dz in near:
            for q in slots[dz]:
                i_copy(par, q, source(q)).wait_recv()
            at = row_block((r + n_row - dz) % n_row)
            h = image[par, :, at]
            coeffs = coeffs + across(h, high[:seen, at])
        ch, cl = split(coeffs)
        c_both = jnp.concatenate([ch, cl], axis=0)

        def residual(at):
            both = jnp.dot(c_both, high[:seen, at], preferred_element_type=f32)
            fix = jnp.dot(ch, low[:seen, at], preferred_element_type=f32)
            return image[par, :, at].astype(f32) - (both[:width] + both[width:] + fix)

        beta_ref[step] = orthonormal(residual, step + 1)
        alpha_ref[step] = coeffs[:, step * width : seen].T
        for q in range(1, groups):
            i_copy(par, q, group).wait_send()

    own = lane_block(group)
    basis_ref[...] = high[:, own].astype(f32) + low[:, own].astype(f32)


def local(impedance, start):
    n_row, n_col = lax.axis_size("row"), lax.axis_size("col")
    share, width = start.shape
    pair = LANES // share
    total = share * n_row * n_col
    groups = total // LANES
    blocks = (STEPS + 1) * width
    member = lax.axis_index("col") % pair
    lanes = lax.broadcasted_iota(jnp.int32, (width, LANES), 1)
    placed = jnp.where(lanes // share == member, jnp.concatenate([start.T] * pair, axis=1), 0.0)
    placed = placed.astype(bf16)
    vmem = pl.BlockSpec(memory_space=pltpu.VMEM)
    dma = pltpu.SemaphoreType.DMA
    basis, alphas, betas = pl.pallas_call(
        functools.partial(kernel, n_row, n_col, pair),
        out_shape=(
            jax.ShapeDtypeStruct((blocks, LANES), f32),
            jax.ShapeDtypeStruct((STEPS, width, width), f32),
            jax.ShapeDtypeStruct((STEPS, width, width), f32),
        ),
        in_specs=[vmem, vmem],
        out_specs=(vmem, vmem, vmem),
        scratch_shapes=[
            pltpu.VMEM((n_col, LANES, impedance.shape[1]), bf16),
            pltpu.VMEM((pair, width, LANES), bf16),
            pltpu.VMEM((width, total), bf16),
            pltpu.VMEM((2, width, total), bf16),
            pltpu.VMEM((blocks, total), bf16),
            pltpu.VMEM((blocks, total), bf16),
            pltpu.VMEM((2, width, total), bf16),
            dma((n_col,)), dma((n_col,)),
            dma((pair,)), dma((pair,)),
            dma((groups,)), dma((groups,)),
            dma((2, groups)), dma((2, groups)),
        ],
        compiler_params=pltpu.CompilerParams(
            collective_id=0, has_side_effects=True, vmem_limit_bytes=60 * 1024 * 1024
        ),
    )(impedance, placed)
    mine = lax.dynamic_slice_in_dim(basis, member * share, share, 1)
    return mine.T, alphas, betas


def solution(mesh):
    return jax.shard_map(
        local,
        mesh=mesh,
        in_specs=(P("row", "col"), P(("row", "col"), None)),
        out_specs=(P(("row", "col"), None), P(), P()),
        check_vma=False,
    )
```

profile of v0, /device:TPU:0, one launch (start us, length us, event | category | flops | bytes accessed | tf_op | source)
XLA Modules:
  0.0 84.3 jit_solution(1625590076021520300)
XLA Ops:
  0.6 0.0 copy-start.2
  0.7 0.7 copy-done.2
  1.4 0.7 fusion.st_ref
  2.0 78.7 %shard_map.49 = (f32[288,128]{1,0:T(8,128)}, f32[8,32,32]{2,1,0:T(8,128)}, f32[8,32,32]{2,1,0:T(8,128)}) custom-call(bf16[512,256]{1,0:T(8,128)(2,1)} %imp_ref.1, bf16[32,128]{1,0:T(8,128)(2,1)} %fusion.st_ref), custom_call_target="tpu_custom_call" | custom-call | tf_op jit(solution)/shard_map/pallas_call | solution.py:235
  80.7 1.0 %dynamic-slice_bitcast_fusion = f32[64,288]{0,1:T(8,128)S(1)} fusion(f32[288,128]{1,0:T(8,128)} %get-tuple-element.6, s32[]{:T(128)S(6)} %select_n.22), kind=kLoop, calls=%fused_computation | loop fusion | bytes 147460 | tf_op jit(solution)/shard_map/transpose | solution.py:262
  81.8 0.0 copy-start.1
  81.8 0.8 copy.5
  82.5 0.1 copy-done.1
  82.7 0.0 copy-start
  82.7 0.7 copy.8
  83.3 0.3 copy-done
  83.6 0.7 copy.9
  (2 shorter events, 0.0 us)
Async XLA Ops:
  0.6 0.7 copy-start.2
  81.8 0.9 %copy-start.1 = (f32[8,32,32]{2,1,0:T(8,128)S(1)}, f32[8,32,32]{2,1,0:T(8,128)}, u32[]{:S(2)}) copy-start(f32[8,32,32]{2,1,0:T(8,128)} %get-tuple-element.18) | copy-start | bytes 98308
  82.7 1.0 %copy-start = (f32[8,32,32]{2,1,0:T(8,128)S(1)}, f32[8,32,32]{2,1,0:T(8,128)}, u32[]{:S(2)}) copy-start(f32[8,32,32]{2,1,0:T(8,128)} %get-tuple-element.19) | copy-start | bytes 98308
where the time goes:
time: 84.5 us; the launch traced here: 84.3 us
  Pallas kernels  78.7 us (93%)
  local copies, waits for them, and re-layouts  4.19 us (5%)
    pallas_call x1, Pallas kernels, local(): pl.pallas_call(functools.partial(kernel, n_row, n_col, pair), out_shape=(...  78.7 us
    unnamed x9, local copies, waits for them, and re-layouts  3.18 us

commit v1 on v0

--- a/solution.py
+++ b/solution.py
@@ -11,6 +11,7 @@
 LANES = 128
 CHUNK = 2048
 PANEL = 16
+PARTS = 2
 MESH = pl.DeviceIdType.MESH
 f32 = jnp.float32
 bf16 = jnp.bfloat16
@@ -56,9 +57,10 @@
 
 def kernel(
     n_row, n_col, pair,
-    imp_ref, st_ref, basis_ref, alpha_ref, beta_ref,
-    slab, parts, begin, image, high, low, res,
-    a_send, a_recv, p_send, p_recv, s_send, s_recv, i_send, i_recv,
+    imp_hbm, st_ref, basis_ref, alpha_ref, beta_ref,
+    imp_ref,
+    slab, tower, relay, parts, begin, image, high, low, res,
+    a_send, a_recv, b_send, b_recv, d_send, d_recv, f_send, f_recv, imp_sem, p_send, p_recv, s_send, s_recv, i_send, i_recv,
 ):
     r = lax.axis_index("row")
     c = lax.axis_index("col")
@@ -74,18 +76,38 @@
     chunk = min(CHUNK, total)
     trips = total // chunk
 
+    load = pltpu.make_async_copy(imp_hbm, imp_ref, imp_sem)
+    load.start()
     barrier = pltpu.get_barrier_semaphore()
     for d in range(1, devices):
         t = (me + d) % devices
         pl.semaphore_signal(barrier, inc=1, device_id=(t // n_col, t % n_col), device_id_type=MESH)
+    load.wait()
     pl.semaphore_wait(barrier, devices - 1)
 
     def lane_block(g):
         return pl.ds(pl.multiple_of(g * LANES, LANES), LANES)
 
     def row_block(k):
-        rows = per_row * LANES
-        return pl.ds(pl.multiple_of(k * rows, rows), rows)
+        size = per_row * LANES
+        return pl.ds(pl.multiple_of(k * size, size), size)
+
+    planes = n_row // 2
+    side, level = r // planes, r % planes
+    rows = imp_ref.shape[0]
+    strips = cb // LANES
+
+    def shift(value, offset, count, sign=1):
+        if count & (count - 1):
+            return (value + sign * offset + count) % count
+        moved, bit = 0, 1
+        while bit < count:
+            moved = moved + (value // bit + offset // bit) % 2 * bit
+            bit *= 2
+        return moved
+
+    def owned(z, x):
+        return (z + x % 2 * planes) % n_row * per_row + x // 2
 
     def p_copy(q, owner):
         return pltpu.make_async_remote_copy(
@@ -113,17 +135,101 @@
             device_id=peer(q), device_id_type=MESH,
         )
 
-    def a_copy(q, owner):
-        t = (c + q) % n_col
-        return pltpu.make_async_remote_copy(
-            src_ref=imp_ref.at[pl.ds(pl.multiple_of((t // pair) * LANES, LANES), LANES), :],
-            dst_ref=slab.at[owner],
-            send_sem=a_send.at[q], recv_sem=a_recv.at[q],
-            device_id=(r, t), device_id_type=MESH,
-        )
-
+    def a_copy(g):
+        return pltpu.make_async_remote_copy(
+            src_ref=imp_ref.at[g * LANES : (g + 1) * LANES, :], dst_ref=slab.at[c],
+            send_sem=a_send.at[g], recv_sem=a_recv.at[c],
+            device_id=(r, 2 * g), device_id_type=MESH,
+        )
+
+    k = c % 2
+    lanes_of = [slice(s * LANES, (s + 1) * LANES) for s in range(strips)]
+    hops = max(planes // 2, 1)
+
+    def strip_target(s):
+        g = c * strips + s
+        return (g // per_row + planes) % n_row, g % per_row * 2 + 1
+
+    def strip_relay(s):
+        z, x = strip_target(s)
+        return x - 1 + z % planes % 2
+
+    def strip_local(s):
+        z, x = strip_target(s)
+        return (z == r) & (x == c)
+
+    def strip_direct(s):
+        z, x = strip_target(s)
+        return ((z // planes == side) | (strip_relay(s) == c)) & jnp.logical_not(strip_local(s))
+
+    def strip_relayed(s):
+        return (strip_target(s)[0] // planes != side) & (strip_relay(s) != c)
+
+    def b_copy(s):
+        return pltpu.make_async_remote_copy(
+            src_ref=imp_ref.at[:, lanes_of[s]], dst_ref=tower.at[r],
+            send_sem=b_send.at[s], recv_sem=b_recv.at[r],
+            device_id=strip_target(s), device_id_type=MESH,
+        )
+
+    def part(i):
+        return slice(i * rows // PARTS, (i + 1) * rows // PARTS)
+
+    def d_copy(s, i):
+        slot = strip_target(s)[0] % planes // 2
+        return pltpu.make_async_remote_copy(
+            src_ref=imp_ref.at[part(i), lanes_of[s]], dst_ref=relay.at[slot, part(i)],
+            send_sem=d_send.at[s, i], recv_sem=d_recv.at[slot, i],
+            device_id=(r, strip_relay(s)), device_id_type=MESH,
+        )
+
+    def relay_target(slot):
+        return (1 - side) * planes + slot * 2 + k, c // 2 * 2 + 1
+
+    def relay_used(slot):
+        z, x = relay_target(slot)
+        g = (z + planes) % n_row * per_row + x // 2
+        return (slot * 2 + k < planes) & (g // strips != c)
+
+    def f_copy(slot, i):
+        return pltpu.make_async_remote_copy(
+            src_ref=relay.at[slot, part(i)], dst_ref=tower.at[r, part(i)],
+            send_sem=f_send.at[slot, i], recv_sem=f_recv.at[r, i],
+            device_id=relay_target(slot), device_id_type=MESH,
+        )
+
+    def d_wait(slot, i):
+        where = relay.at[slot, part(i)]
+        pltpu.make_async_remote_copy(
+            src_ref=where, dst_ref=where, send_sem=f_send.at[slot, i], recv_sem=d_recv.at[slot, i],
+            device_id=(r, c), device_id_type=MESH,
+        ).wait_recv()
+
+    def send_strip(s):
+        for i in range(PARTS):
+            d_copy(s, i).start()
+
+    def sent_strip(s):
+        for i in range(PARTS):
+            d_copy(s, i).wait_send()
+
+    def passed_on(slot):
+        for i in range(PARTS):
+            f_copy(slot, i).wait_send()
+
+    def pass_on(slot, i):
+        d_wait(slot, i)
+        f_copy(slot, i).start()
+
+    mine_at = owned(r, c)
+    even = c % 2 == 0
+
+    for s in range(strips):
+        pl.when(strip_relayed(s))(functools.partial(send_strip, s))
     for q in range(1, pair):
         p_copy(q, member).start()
+    for s in range(strips):
+        pl.when(strip_direct(s))(b_copy(s).start)
     parts[member] = st_ref[...]
     for q in range(1, pair):
         p_copy(q, (member - q + pair) % pair).wait_recv()
@@ -133,9 +239,21 @@
     begin[:, lane_block(group)] = whole
     for q in near_first:
         st_copy(q, group).start()
-    for q in range(1, n_col):
-        a_copy(q, c).start()
-    slab[c] = imp_ref[pl.ds(pl.multiple_of((c // pair) * LANES, LANES), LANES), :]
+    for g in range(per_row):
+        pl.when(c != 2 * g)(a_copy(g).start)
+    for g in range(per_row):
+        @pl.when(c == 2 * g)
+        def _():
+            slab[c] = imp_ref[g * LANES : (g + 1) * LANES, :]
+
+    for s in range(strips):
+        @pl.when(strip_local(s))
+        def _():
+            tower[r] = imp_ref[:, lanes_of[s]]
+
+    for i in range(PARTS):
+        for slot in range(hops):
+            pl.when(relay_used(slot))(functools.partial(pass_on, slot, i))
     for q in range(1, groups):
         st_copy(q, source(q)).wait_recv()
 
@@ -169,39 +287,100 @@
         return begin[:, at].astype(f32)
 
     orthonormal(first, 0)
-    for q in range(1, n_col):
-        a_copy(q, (c - q + n_col) % n_col).wait_recv()
+
+    def a_wait(x):
+        pltpu.make_async_remote_copy(
+            src_ref=slab.at[x], dst_ref=slab.at[x], send_sem=a_send.at[0], recv_sem=a_recv.at[x],
+            device_id=(r, x), device_id_type=MESH,
+        ).wait_recv()
+
+    def b_wait(z):
+        pltpu.make_async_remote_copy(
+            src_ref=tower.at[z], dst_ref=tower.at[z], send_sem=b_send.at[0], recv_sem=b_recv.at[z],
+            device_id=(z, c), device_id_type=MESH,
+        ).wait_recv()
+
+    for x in range(n_col):
+        pl.when(even & (c != x))(functools.partial(a_wait, x))
+
+    def t_wait(z, i):
+        where = tower.at[z, part(i)]
+        pltpu.make_async_remote_copy(
+            src_ref=where, dst_ref=where, send_sem=f_send.at[0, i], recv_sem=f_recv.at[z, i],
+            device_id=(z, c), device_id_type=MESH,
+        ).wait_recv()
+
+    def t_waits(z):
+        for i in range(PARTS):
+            t_wait(z, i)
+
+    helper = c - 1 + level % 2
+    for z in range(n_row):
+        source = mine_at // strips
+        far = (z // planes != side) & (source != helper)
+        here = (source == c) & (z == r)
+        pl.when((k == 1) & far)(functools.partial(t_waits, z))
+        pl.when((k == 1) & jnp.logical_not(far) & jnp.logical_not(here))(functools.partial(b_wait, z))
     for q in range(1, pair):
         p_copy(q, member).wait_send()
     for q in range(1, groups):
         st_copy(q, group).wait_send()
-    for q in range(1, n_col):
-        a_copy(q, c).wait_send()
-
-    def i_copy(par, q, owner):
+    for g in range(per_row):
+        pl.when(c != 2 * g)(a_copy(g).wait_send)
+    for s in range(strips):
+        pl.when(strip_direct(s))(b_copy(s).wait_send)
+        pl.when(strip_relayed(s))(functools.partial(sent_strip, s))
+    for slot in range(hops):
+        pl.when(relay_used(slot))(functools.partial(passed_on, slot))
+
+    offsets = [(dz, dc) for dz in reversed(range(planes)) for dc in reversed(range(n_col)) if dz or dc]
+
+    def i_copy(par, dz, dc, owner):
         where = image.at[par, :, lane_block(owner)]
+        index = dz * n_col + dc
         return pltpu.make_async_remote_copy(
             src_ref=where, dst_ref=where,
-            send_sem=i_send.at[par, q], recv_sem=i_recv.at[par, q],
-            device_id=peer(q), device_id_type=MESH,
-        )
+            send_sem=i_send.at[par, index], recv_sem=i_recv.at[par, index],
+            device_id=(side * planes + shift(level, dz, planes), shift(c, dc, n_col)),
+            device_id_type=MESH,
+        )
+
+    def i_wait(par, dz, dc):
+        z = side * planes + shift(level, dz, planes, -1)
+        i_copy(par, dz, dc, owned(z, shift(c, dc, n_col, -1))).wait_recv()
 
     for step in range(STEPS):
         par = step % 2
         seen = (step + 1) * width
-        mine = jnp.zeros((width, LANES), f32)
-        for k in range(n_col):
-            mine = mine + across(high[step * width : seen, k * cb : (k + 1) * cb], slab[k])
-        image[par, :, lane_block(group)] = mine.astype(image.dtype)
-        for q in near_first:
-            i_copy(par, q, group).start()
+        now = slice(step * width, seen)
+
+        @pl.when(even)
+        def _():
+            mine = jnp.zeros((width, LANES), f32)
+            for x in range(n_col):
+                mine = mine + across(high[now, x * cb : (x + 1) * cb], slab[x])
+            image[par, :, lane_block(mine_at)] = mine.astype(image.dtype)
+
+        @pl.when(c % 2 == 1)
+        def _():
+            mine = jnp.zeros((width, LANES), f32)
+            for z in range(n_row):
+                mine = mine + jnp.dot(
+                    high[now, z * rows : (z + 1) * rows], tower[z], preferred_element_type=f32
+                )
+            image[par, :, lane_block(mine_at)] = mine.astype(image.dtype)
+
+        for dz, dc in offsets:
+            i_copy(par, dz, dc, mine_at).start()
         coeffs = jnp.zeros((width, seen), f32)
-        for dz in near:
-            for q in slots[dz]:
-                i_copy(par, q, source(q)).wait_recv()
-            at = row_block((r + n_row - dz) % n_row)
-            h = image[par, :, at]
-            coeffs = coeffs + across(h, high[:seen, at])
+        for dz in range(planes):
+            for there in [dc for z, dc in reversed(offsets) if z == dz]:
+                i_wait(par, dz, there)
+            base = shift(level, dz, planes, -1)
+            for half in range(2):
+                at = row_block(base + half * planes)
+                h = image[par, :, at]
+                coeffs = coeffs + across(h, high[:seen, at]) + across(h, low[:seen, at])
         ch, cl = split(coeffs)
         c_both = jnp.concatenate([ch, cl], axis=0)
 
@@ -212,8 +391,8 @@
 
         beta_ref[step] = orthonormal(residual, step + 1)
         alpha_ref[step] = coeffs[:, step * width : seen].T
-        for q in range(1, groups):
-            i_copy(par, q, group).wait_send()
+        for dz, dc in offsets:
+            i_copy(par, dz, dc, mine_at).wait_send()
 
     own = lane_block(group)
     basis_ref[...] = high[:, own].astype(f32) + low[:, own].astype(f32)
@@ -230,6 +409,7 @@
     lanes = lax.broadcasted_iota(jnp.int32, (width, LANES), 1)
     placed = jnp.where(lanes // share == member, jnp.concatenate([start.T] * pair, axis=1), 0.0)
     placed = placed.astype(bf16)
+    hops = max(n_row // 4, 1)
     vmem = pl.BlockSpec(memory_space=pltpu.VMEM)
     dma = pltpu.SemaphoreType.DMA
     basis, alphas, betas = pl.pallas_call(
@@ -239,17 +419,23 @@
             jax.ShapeDtypeStruct((STEPS, width, width), f32),
             jax.ShapeDtypeStruct((STEPS, width, width), f32),
         ),
-        in_specs=[vmem, vmem],
+        in_specs=[pl.BlockSpec(memory_space=pl.ANY), vmem],
         out_specs=(vmem, vmem, vmem),
         scratch_shapes=[
+            pltpu.VMEM(impedance.shape, bf16),
             pltpu.VMEM((n_col, LANES, impedance.shape[1]), bf16),
+            pltpu.VMEM((n_row, impedance.shape[0], LANES), bf16),
+            pltpu.VMEM((hops, impedance.shape[0], LANES), bf16),
             pltpu.VMEM((pair, width, LANES), bf16),
             pltpu.VMEM((width, total), bf16),
             pltpu.VMEM((2, width, total), bf16),
             pltpu.VMEM((blocks, total), bf16),
             pltpu.VMEM((blocks, total), bf16),
             pltpu.VMEM((2, width, total), bf16),
-            dma((n_col,)), dma((n_col,)),
+            dma((n_col // 2,)), dma((n_col,)),
+            dma((impedance.shape[1] // LANES,)), dma((n_row,)),
+            dma((impedance.shape[1] // LANES, PARTS)), dma((hops, PARTS)),
+            dma((hops, PARTS)), dma((n_row, PARTS)), dma,
             dma((pair,)), dma((pair,)),
             dma((groups,)), dma((groups,)),
             dma((2, groups)), dma((2, groups)),

time: 84.5 us -> 78.4 us (0.928)
  Pallas kernels: 78.7 us -> 72.5 us
    pallas_call x1, Pallas kernels: 78.7 us -> 72.5 us  [local(): pl.pallas_call(functools.partial(kernel, n_row, n_col, pair), out_shape=(...]
where the time goes in v1:
time: 78.4 us; the launch traced here: 78.1 us
  Pallas kernels  72.5 us (92%)
  local copies, waits for them, and re-layouts  4.19 us (5%)
    pallas_call x1, Pallas kernels, local(): pl.pallas_call(functools.partial(kernel, n_row, n_col, pair), out_shape=(...  72.5 us
    unnamed x9, local copies, waits for them, and re-layouts  3.18 us

profile of v1, /device:TPU:0, one launch (start us, length us, event | category | flops | bytes accessed | tf_op | source)
XLA Modules:
  0.0 78.1 jit_solution(9323524399513252515)
XLA Ops:
  0.6 0.0 copy-start.2
  0.7 0.7 copy-done.2
  1.4 0.7 fusion.st_ref
  2.0 72.5 %shard_map.49 = (f32[288,128]{1,0:T(8,128)}, f32[8,32,32]{2,1,0:T(8,128)}, f32[8,32,32]{2,1,0:T(8,128)}) custom-call(bf16[512,256]{1,0:T(8,128)(2,1)} %imp_hbm.1, bf16[32,128]{1,0:T(8,128)(2,1)} %fusion.st_ref), custom_call_target="tpu_custom_call" | custom-call | tf_op jit(solution)/shard_map/pallas_call | solution.py:415
  74.5 1.0 %dynamic-slice_bitcast_fusion = f32[64,288]{0,1:T(8,128)S(1)} fusion(f32[288,128]{1,0:T(8,128)} %get-tuple-element.6, s32[]{:T(128)S(6)} %select_n.22), kind=kLoop, calls=%fused_computation | loop fusion | bytes 147460 | tf_op jit(solution)/shard_map/transpose | solution.py:448
  75.6 0.0 copy-start.1
  75.6 0.8 copy.5
  76.3 0.1 copy-done.1
  76.5 0.0 copy-start
  76.5 0.7 copy.8
  77.1 0.3 copy-done
  77.4 0.7 copy.9
  (2 shorter events, 0.0 us)
Async XLA Ops:
  0.6 0.7 copy-start.2
  75.6 0.9 %copy-start.1 = (f32[8,32,32]{2,1,0:T(8,128)S(1)}, f32[8,32,32]{2,1,0:T(8,128)}, u32[]{:S(2)}) copy-start(f32[8,32,32]{2,1,0:T(8,128)} %get-tuple-element.18) | copy-start | bytes 98308
  76.5 1.0 %copy-start = (f32[8,32,32]{2,1,0:T(8,128)S(1)}, f32[8,32,32]{2,1,0:T(8,128)}, u32[]{:S(2)}) copy-start(f32[8,32,32]{2,1,0:T(8,128)} %get-tuple-element.19) | copy-start | bytes 98308

commit v2 on v1

--- a/solution.py
+++ b/solution.py
@@ -57,8 +57,8 @@
 
 def kernel(
     n_row, n_col, pair,
-    imp_hbm, st_ref, basis_ref, alpha_ref, beta_ref,
-    imp_ref,
+    imp_hbm, start_ref, basis_ref, alpha_ref, beta_ref,
+    imp_ref, st_ref,
     slab, tower, relay, parts, begin, image, high, low, res,
     a_send, a_recv, b_send, b_recv, d_send, d_recv, f_send, f_recv, imp_sem, p_send, p_recv, s_send, s_recv, i_send, i_recv,
 ):
@@ -70,7 +70,7 @@
     me = r * n_col + c
     group = r * per_row + c // pair
     member = c % pair
-    width = st_ref.shape[0]
+    width, share = start_ref.shape
     cb = imp_ref.shape[1]
     total = image.shape[2]
     chunk = min(CHUNK, total)
@@ -82,6 +82,10 @@
     for d in range(1, devices):
         t = (me + d) % devices
         pl.semaphore_signal(barrier, inc=1, device_id=(t // n_col, t % n_col), device_id_type=MESH)
+    turned = start_ref[...]
+    lanes = lax.broadcasted_iota(jnp.int32, (width, LANES), 1)
+    placed = jnp.where(lanes // share == member, jnp.concatenate([turned] * pair, axis=1), 0.0)
+    st_ref[...] = placed.astype(bf16)
     load.wait()
     pl.semaphore_wait(barrier, devices - 1)
 
@@ -106,8 +110,13 @@
             bit *= 2
         return moved
 
+    share_of = per_row // planes
+
     def owned(z, x):
-        return (z + x % 2 * planes) % n_row * per_row + x // 2
+        q = x // 2
+        far = (1 - z // planes) * planes + q % planes
+        other = far * per_row + z % planes * share_of + q // planes
+        return x % 2 * other + (1 - x % 2) * (z * per_row + q)
 
     def p_copy(q, owner):
         return pltpu.make_async_remote_copy(
@@ -148,7 +157,9 @@
 
     def strip_target(s):
         g = c * strips + s
-        return (g // per_row + planes) % n_row, g % per_row * 2 + 1
+        z, at = g // per_row, g % per_row
+        q = at % share_of * planes + z % planes
+        return (1 - z // planes) * planes + at // share_of, q * 2 + 1
 
     def strip_relay(s):
         z, x = strip_target(s)
@@ -187,9 +198,7 @@
         return (1 - side) * planes + slot * 2 + k, c // 2 * 2 + 1
 
     def relay_used(slot):
-        z, x = relay_target(slot)
-        g = (z + planes) % n_row * per_row + x // 2
-        return (slot * 2 + k < planes) & (g // strips != c)
+        return (slot * 2 + k < planes) & (owned(*relay_target(slot)) // strips != c)
 
     def f_copy(slot, i):
         return pltpu.make_async_remote_copy(
@@ -349,6 +358,15 @@
         z = side * planes + shift(level, dz, planes, -1)
         i_copy(par, dz, dc, owned(z, shift(c, dc, n_col, -1))).wait_recv()
 
+    def turn(index):
+        at = slice(index * width, (index + 1) * width)
+        own = lane_block(group)
+        value = high[at, own].astype(f32) + low[at, own].astype(f32)
+        out = value[:, :share]
+        for i in range(1, pair):
+            out = jnp.where(member == i, value[:, i * share : (i + 1) * share], out)
+        basis_ref[at, :] = out
+
     for step in range(STEPS):
         par = step % 2
         seen = (step + 1) * width
@@ -372,13 +390,18 @@
 
         for dz, dc in offsets:
             i_copy(par, dz, dc, mine_at).start()
+        turn(step)
         coeffs = jnp.zeros((width, seen), f32)
         for dz in range(planes):
             for there in [dc for z, dc in reversed(offsets) if z == dz]:
                 i_wait(par, dz, there)
             base = shift(level, dz, planes, -1)
-            for half in range(2):
-                at = row_block(base + half * planes)
+            spots = [row_block(side * planes + base)]
+            size = share_of * LANES
+            for i in range(planes):
+                far = ((1 - side) * planes + i) * per_row + base * share_of
+                spots.append(pl.ds(pl.multiple_of(far * LANES, size), size))
+            for at in spots:
                 h = image[par, :, at]
                 coeffs = coeffs + across(h, high[:seen, at]) + across(h, low[:seen, at])
         ch, cl = split(coeffs)
@@ -394,8 +417,7 @@
         for dz, dc in offsets:
             i_copy(par, dz, dc, mine_at).wait_send()
 
-    own = lane_block(group)
-    basis_ref[...] = high[:, own].astype(f32) + low[:, own].astype(f32)
+    turn(STEPS)
 
 
 def local(impedance, start):
@@ -405,17 +427,13 @@
     total = share * n_row * n_col
     groups = total // LANES
     blocks = (STEPS + 1) * width
-    member = lax.axis_index("col") % pair
-    lanes = lax.broadcasted_iota(jnp.int32, (width, LANES), 1)
-    placed = jnp.where(lanes // share == member, jnp.concatenate([start.T] * pair, axis=1), 0.0)
-    placed = placed.astype(bf16)
     hops = max(n_row // 4, 1)
     vmem = pl.BlockSpec(memory_space=pltpu.VMEM)
     dma = pltpu.SemaphoreType.DMA
     basis, alphas, betas = pl.pallas_call(
         functools.partial(kernel, n_row, n_col, pair),
         out_shape=(
-            jax.ShapeDtypeStruct((blocks, LANES), f32),
+            jax.ShapeDtypeStruct((blocks, share), f32),
             jax.ShapeDtypeStruct((STEPS, width, width), f32),
             jax.ShapeDtypeStruct((STEPS, width, width), f32),
         ),
@@ -423,6 +441,7 @@
         out_specs=(vmem, vmem, vmem),
         scratch_shapes=[
             pltpu.VMEM(impedance.shape, bf16),
+            pltpu.VMEM((width, LANES), bf16),
             pltpu.VMEM((n_col, LANES, impedance.shape[1]), bf16),
             pltpu.VMEM((n_row, impedance.shape[0], LANES), bf16),
             pltpu.VMEM((hops, impedance.shape[0], LANES), bf16),
@@ -443,9 +462,8 @@
         compiler_params=pltpu.CompilerParams(
             collective_id=0, has_side_effects=True, vmem_limit_bytes=60 * 1024 * 1024
         ),
-    )(impedance, placed)
-    mine = lax.dynamic_slice_in_dim(basis, member * share, share, 1)
-    return mine.T, alphas, betas
+    )(impedance, start.T)
+    return basis.T, alphas, betas
 
 
 def solution(mesh):

time: 78.4 us -> 74.9 us (0.955)
  Pallas kernels: 72.5 us -> 70.7 us
  local copies, waits for them, and re-layouts: 4.19 us -> 3.31 us
    pallas_call x1, Pallas kernels: 72.5 us -> 70.7 us  [local(): pl.pallas_call(functools.partial(kernel, n_row, n_col, pair), out_shape=(...]
    transpose x1 -> x0, local copies, waits for them, and re-layouts: 1.01 us -> none  [local(): return (mine.T, alphas, betas)]
    unnamed x9 -> x7, local copies, waits for them, and re-layouts: 3.18 us -> 3.31 us
where the time goes in v2:
time: 74.9 us; the launch traced here: 74.7 us
  Pallas kernels  70.7 us (94%)
  local copies, waits for them, and re-layouts  3.31 us (4%)
    pallas_call x1, Pallas kernels, local(): pl.pallas_call(functools.partial(kernel, n_row, n_col, pair), out_shape=(...  70.7 us
    unnamed x7, local copies, waits for them, and re-layouts  3.31 us

profile of v2, /device:TPU:0, one launch (start us, length us, event | category | flops | bytes accessed | tf_op | source)
XLA Modules:
  0.0 74.7 jit_solution(1823971815767319509)
XLA Ops:
  0.6 70.7 %shard_map.49 = (f32[288,64]{1,0:T(8,128)}, f32[8,32,32]{2,1,0:T(8,128)}, f32[8,32,32]{2,1,0:T(8,128)}) custom-call(bf16[512,256]{1,0:T(8,128)(2,1)} %imp_hbm.1, f32[32,64]{1,0:T(8,128)} %bitcast.3), custom_call_target="tpu_custom_call" | custom-call | tf_op jit(solution)/shard_map/pallas_call | solution.py:433
  71.4 0.0 copy-start.1
  71.4 1.7 %copy.5 = f32[64,288]{1,0:T(8,128)} copy(f32[64,288]{0,1:T(8,128)} %bitcast.2) | data formatting | bytes 147456
  73.1 0.0 copy-done.1
  73.1 0.0 copy-start
  73.1 0.7 copy.8
  73.8 0.3 copy-done
  74.1 0.7 copy.9
Async XLA Ops:
  71.4 1.7 %copy-start.1 = (f32[8,32,32]{2,1,0:T(8,128)S(1)}, f32[8,32,32]{2,1,0:T(8,128)}, u32[]{:S(2)}) copy-start(f32[8,32,32]{2,1,0:T(8,128)} %get-tuple-element.16) | copy-start | bytes 98308
  73.1 1.0 %copy-start = (f32[8,32,32]{2,1,0:T(8,128)S(1)}, f32[8,32,32]{2,1,0:T(8,128)}, u32[]{:S(2)}) copy-start(f32[8,32,32]{2,1,0:T(8,128)} %get-tuple-element.17) | copy-start | bytes 98308

commit v3 on v2

--- a/solution.py
+++ b/solution.py
@@ -237,8 +237,6 @@
         pl.when(strip_relayed(s))(functools.partial(send_strip, s))
     for q in range(1, pair):
         p_copy(q, member).start()
-    for s in range(strips):
-        pl.when(strip_direct(s))(b_copy(s).start)
     parts[member] = st_ref[...]
     for q in range(1, pair):
         p_copy(q, (member - q + pair) % pair).wait_recv()
@@ -248,6 +246,8 @@
     begin[:, lane_block(group)] = whole
     for q in near_first:
         st_copy(q, group).start()
+    for s in range(strips):
+        pl.when(strip_direct(s))(b_copy(s).start)
     for g in range(per_row):
         pl.when(c != 2 * g)(a_copy(g).start)
     for g in range(per_row):
@@ -311,6 +311,14 @@
 
     for x in range(n_col):
         pl.when(even & (c != x))(functools.partial(a_wait, x))
+
+    @pl.when(even)
+    def _():
+        for x in range(n_col):
+            for i in range(0, cb, LANES):
+                spot = x * cb + i
+                tower[spot // rows, spot % rows : spot % rows + LANES, :] = slab[x, :, i : i + LANES].T
+
 
     def t_wait(z, i):
         where = tower.at[z, part(i)]
@@ -343,6 +351,7 @@
         pl.when(relay_used(slot))(functools.partial(passed_on, slot))
 
     offsets = [(dz, dc) for dz in reversed(range(planes)) for dc in reversed(range(n_col)) if dz or dc]
+    offsets.sort(key=lambda to: (-to[0] - (to[1] // 2).bit_count(), to[0], -to[1]))
 
     def i_copy(par, dz, dc, owner):
         where = image.at[par, :, lane_block(owner)]
@@ -372,22 +381,12 @@
         seen = (step + 1) * width
         now = slice(step * width, seen)
 
-        @pl.when(even)
-        def _():
-            mine = jnp.zeros((width, LANES), f32)
-            for x in range(n_col):
-                mine = mine + across(high[now, x * cb : (x + 1) * cb], slab[x])
-            image[par, :, lane_block(mine_at)] = mine.astype(image.dtype)
-
-        @pl.when(c % 2 == 1)
-        def _():
-            mine = jnp.zeros((width, LANES), f32)
-            for z in range(n_row):
-                mine = mine + jnp.dot(
-                    high[now, z * rows : (z + 1) * rows], tower[z], preferred_element_type=f32
-                )
-            image[par, :, lane_block(mine_at)] = mine.astype(image.dtype)
-
+        mine = jnp.zeros((width, LANES), f32)
+        for z in range(n_row):
+            mine = mine + jnp.dot(
+                high[now, z * rows : (z + 1) * rows], tower[z], preferred_element_type=f32
+            )
+        image[par, :, lane_block(mine_at)] = mine.astype(image.dtype)
         for dz, dc in offsets:
             i_copy(par, dz, dc, mine_at).start()
         turn(step)

time: 74.9 us -> 74.3 us (level)
  no operation moved by 1% of the time
where the time goes in v3:
time: 74.3 us; the launch traced here: 74.1 us
  Pallas kernels  70.1 us (94%)
  local copies, waits for them, and re-layouts  3.31 us (4%)
    pallas_call x1, Pallas kernels, local(): pl.pallas_call(functools.partial(kernel, n_row, n_col, pair), out_shape=(...  70.1 us
    unnamed x7, local copies, waits for them, and re-layouts  3.31 us

profile of v3, /device:TPU:0, one launch (start us, length us, event | category | flops | bytes accessed | tf_op | source)
XLA Modules:
  0.0 74.1 jit_solution(5364935698604548650)
XLA Ops:
  0.6 70.1 %shard_map.49 = (f32[288,64]{1,0:T(8,128)}, f32[8,32,32]{2,1,0:T(8,128)}, f32[8,32,32]{2,1,0:T(8,128)}) custom-call(bf16[512,256]{1,0:T(8,128)(2,1)} %imp_hbm.1, f32[32,64]{1,0:T(8,128)} %bitcast.3), custom_call_target="tpu_custom_call" | custom-call | tf_op jit(solution)/shard_map/pallas_call | solution.py:432
  70.7 0.0 copy-start.1
  70.8 1.7 %copy.5 = f32[64,288]{1,0:T(8,128)} copy(f32[64,288]{0,1:T(8,128)} %bitcast.2) | data formatting | bytes 147456
  72.5 0.0 copy-done.1
  72.5 0.0 copy-start
  72.5 0.7 copy.8
  73.1 0.3 copy-done
  73.4 0.7 copy.9
Async XLA Ops:
  70.7 1.7 %copy-start.1 = (f32[8,32,32]{2,1,0:T(8,128)S(1)}, f32[8,32,32]{2,1,0:T(8,128)}, u32[]{:S(2)}) copy-start(f32[8,32,32]{2,1,0:T(8,128)} %get-tuple-element.16) | copy-start | bytes 98308
  72.5 1.0 %copy-start = (f32[8,32,32]{2,1,0:T(8,128)S(1)}, f32[8,32,32]{2,1,0:T(8,128)}, u32[]{:S(2)}) copy-start(f32[8,32,32]{2,1,0:T(8,128)} %get-tuple-element.17) | copy-start | bytes 98308
